TPU v7x, 32 devices: a whole 2x2x4 slice. The times are simulated.
32 devices in a mesh: ctx: 16 (over z, x, core), tp: 2 (over y).
Axes of the slice: x: 2, y: 2, z: 4, core: 2. Of those that a mesh axis runs over, the one named last changes fastest.
Arguments:
- queries: bfloat16 [4096, 8192], P('ctx', 'tp'), may hold values from -6 to 6
- keys: bfloat16 [4096, 1024], P('ctx', 'tp'), may hold values from -6 to 6
- values: bfloat16 [4096, 1024], P('ctx', 'tp'), may hold values from -6 to 6
- documents: int32 [4096], replicated, may hold values from 0 to 3, never falling along the last dimension, each value on 1 to 2048 neighbouring positions
- hist_q: float32 [16, 64], P(None, 'tp'), may hold values from 0.75 to 5.4
- hist_kv: float32 [2, 16, 8], P(None, None, 'tp'), may hold values from 0.75 to 5.4
- out_weight: bfloat16 [8192, 8192], P(('tp', 'ctx')), may hold values from -0.0625 to 0.0625
Outputs:
- mixed: bfloat16 [4096, 8192], P('ctx', 'tp')
- new_hist_q: float32 [16, 64], P(None, 'tp')
- new_hist_kv: float32 [2, 16, 8], P(None, None, 'tp')
All inputs are finite; a program needn't handle non-finite values.
Results may differ from a plain program's by a relative error of at most 0.015.
Values may be sent and summed in bfloat16 or wider, within the bound.
A program may use at most 192 MiB of HBM per device.

v0:
```python
import math

import jax
import jax.numpy as jnp
from jax import lax
from jax.sharding import PartitionSpec as P


def on_device(queries, keys, values, documents, hist_q, hist_kv, out_weight):
    rows_here, width = queries.shape
    kv_heads = hist_kv.shape[2]
    heads_here = hist_q.shape[1]
    group = heads_here // kv_heads
    head_size = width // heads_here
    scale = 1.0 / math.sqrt(head_size)
    query_limit = jnp.max(hist_q, axis=0).reshape(kv_heads, group)
    pair_limit = jnp.max(hist_kv, axis=1)
    raw_query = queries.astype(jnp.float32).reshape(rows_here, kv_heads, group, head_size)
    clipped = jnp.clip(
        raw_query, -query_limit[None, :, :, None], query_limit[None, :, :, None]
    ).astype(jnp.bfloat16)
    query_peak = jnp.max(jnp.abs(raw_query.reshape(rows_here, heads_here, head_size)), axis=(0, 2))
    key_peak = jnp.max(
        jnp.abs(keys.astype(jnp.float32).reshape(rows_here, kv_heads, head_size)), axis=(0, 2)
    )
    value_peak = jnp.max(
        jnp.abs(values.astype(jnp.float32).reshape(rows_here, kv_heads, head_size)), axis=(0, 2)
    )
    current_query, current_pair = lax.pmax((query_peak, jnp.stack([key_peak, value_peak])), "ctx")
    query_start = lax.axis_index("ctx") * rows_here
    query_docs = lax.dynamic_slice_in_dim(documents, query_start, rows_here)
    query_pos = query_start + jnp.arange(rows_here, dtype=jnp.int32)

    def attend(state, key_block, value_block, key_start):
        top, total, acc = state
        count = key_block.shape[0]
        key_float = key_block.astype(jnp.float32).reshape(count, kv_heads, head_size)
        value_float = value_block.astype(jnp.float32).reshape(count, kv_heads, head_size)
        key_clip = jnp.clip(
            key_float, -pair_limit[0][None, :, None], pair_limit[0][None, :, None]
        ).astype(jnp.bfloat16)
        value_clip = jnp.clip(
            value_float, -pair_limit[1][None, :, None], pair_limit[1][None, :, None]
        ).astype(jnp.bfloat16)
        scores = (
            jnp.einsum("tgjd,bgd->gjtb", clipped, key_clip, preferred_element_type=jnp.float32)
            * scale
        )
        key_pos = key_start + jnp.arange(count, dtype=jnp.int32)
        key_docs = lax.dynamic_slice_in_dim(documents, key_start, count)
        allowed = (key_pos[None, :] <= query_pos[:, None]) & (
            key_docs[None, :] == query_docs[:, None]
        )
        new_top = jnp.maximum(top, jnp.max(jnp.where(allowed, scores, -1e30), axis=-1))
        weights = jnp.where(allowed, jnp.exp(scores - new_top[..., None]), 0.0)
        decay = jnp.exp(top - new_top)
        total = total * decay + jnp.sum(weights, axis=-1)
        acc = acc * decay[..., None] + jnp.einsum(
            "gjtb,bgd->gjtd",
            weights.astype(jnp.bfloat16),
            value_clip,
            preferred_element_type=jnp.float32,
        )
        return (new_top, total, acc)

    start_state = (
        jnp.full((kv_heads, group, rows_here), -1e30, jnp.float32),
        jnp.zeros((kv_heads, group, rows_here), jnp.float32),
        jnp.zeros((kv_heads, group, rows_here, head_size), jnp.float32),
    )
    key_piece = lax.all_gather(keys, "ctx", axis=0, tiled=True)
    value_piece = lax.all_gather(values, "ctx", axis=0, tiled=True)
    count = key_piece.shape[0]
    block = 512

    def inner(number, attn_state):
        key_block = lax.dynamic_slice_in_dim(key_piece, number * block, block)
        value_block = lax.dynamic_slice_in_dim(value_piece, number * block, block)
        key_start = number * block
        attn_state = attend(attn_state, key_block, value_block, key_start)
        return attn_state

    top, total, acc = lax.fori_loop(0, count // block, inner, start_state)
    attn = (
        jnp.transpose(acc / total[..., None], (2, 0, 1, 3))
        .reshape(rows_here, width)
        .astype(jnp.bfloat16)
    )
    new_hist_q = jnp.concatenate([current_query[None], hist_q[:-1]], axis=0)
    new_hist_kv = jnp.concatenate([current_pair[:, None], hist_kv[:, :-1]], axis=1)
    partial_rows = jnp.dot(
        attn,
        lax.all_gather(out_weight, "ctx", axis=0, tiled=True),
        preferred_element_type=jnp.float32,
    )
    mixed = lax.psum_scatter(
        partial_rows.astype(jnp.bfloat16), "tp", scatter_dimension=1, tiled=True
    )
    return (mixed, new_hist_q, new_hist_kv)


def solution(mesh):
    in_specs = (
        P("ctx", "tp"),
        P("ctx", "tp"),
        P("ctx", "tp"),
        P(),
        P(None, "tp"),
        P(None, None, "tp"),
        P(("tp", "ctx"), None),
    )
    out_specs = (P("ctx", "tp"), P(None, "tp"), P(None, None, "tp"))
    return jax.shard_map(
        on_device, mesh=mesh, in_specs=in_specs, out_specs=out_specs, check_vma=False
    )
```

profile of v0, /device:TPU:0, one launch (start us, length us, event | category | flops | bytes accessed | tf_op | source)
XLA Modules:
  0.0 530.1 jit_solution(18043814594572523001)
XLA Ops:
  19.6 43.7 %all-gather.4.cloned.1.call-done = bf16[4096,512]{1,0:T(8,128)(2,1)} async-done(((bf16[256,512]{1,0:T(8,128)(2,1)}), bf16[4096,512]{1,0:T(8,128)(2,1)}) %all-gather.4.cloned.1.call-update) | async-done | bytes 4194320 | tf_op jit(solution)/shard_map/all_gather | solution.py:71
  63.3 51.1 %all-gather.6.cloned.1.call-done = bf16[4096,512]{1,0:T(8,128)(2,1)} async-done(((bf16[256,512]{1,0:T(8,128)(2,1)}), bf16[4096,512]{1,0:T(8,128)(2,1)}) %all-gather.6.cloned.1.call-update) | async-done | bytes 4194320 | tf_op jit(solution)/shard_map/all_gather | solution.py:72
  114.4 244.9 %while.19 = (s32[]{:T(128)}, f32[4,8,256]{2,1,0:T(8,128)S(1)}, f32[4,8,256]{2,1,0:T(8,128)S(1)}, f32[4,8,256,128]{3,2,1,0:T(8,128)}, s32[4096]{0:T(1024)}, /*ind...) while((s32[]{:T(128)}, f32[4,8,256]{2,1,0:T(8,128)S(1)}, ...), condition=%wide.region_5.6_spmd.clone, body=%wide.region_2.5_spmd.clone.sunk | while | flops 2199298816 | bytes 65025316 | solution.py:83
  116.7 9.5 %fusion.42 = (f32[4,8,256]{2,1,0:T(8,128)S(1)}, f32[4,512,256,8]{2,1,3,0:T(8,128)}) fusion(pred[256,512]{0,1:T(8,128)(4,1)S(1)} %compare_and_fusion.2, bf16[256,4,8,128]{3,0,2,1:T(8,128)(2,1)S(1)} %get-tuple-element.489, bf16[64,4,8,128]{3,2,1,0:T(8,128)(2,1)S(1)} %get-tuple-element.438, bf16[4]{0:T(256)(128)(2,1)S(1)} %bitcast.109, ...), kind=kOutput, calls=%fused_computation.3.clone.1 | convolution fusion | flops 1087889408 | bytes 19562512 | tf_op jit(solution)/shard_map/while/body/eval_jaxpr/tgjd,bgd->gjtb/dot_general | solution.py:46
  126.2 9.2 %fusion.43 = f32[4,8,256]{2,1,0:T(8,128)S(1)} fusion(f32[4,512,256,8]{2,1,3,0:T(8,128)} %get-tuple-element.441, f32[4,8,256]{2,1,0:T(8,128)S(1)} %select_maximum_fusion.2, pred[256,512]{0,1:T(8,128)(4,1)S(1)} %compare_and_fusion.2), kind=kLoop, calls=%fused_computation.7.clone.1 | loop fusion | flops 16769024 | bytes 16973824 | tf_op jit(solution)/shard_map/while/body/eval_jaxpr/reduce_sum | solution.py:57
  135.4 10.3 %fusion.45 = f32[4,8,256,128]{3,2,1,0:T(8,128)} fusion(f32[4,8,256,128]{3,2,1,0:T(8,128)} %get-tuple-element.466, f32[4,8,256]{2,1,0:T(8,128)S(1)} %get-tuple-element.443, pred[]{:T(512)S(6)} %compare.3, f32[4,512,256,8]{2,1,3,0:T(8,128)} %get-tuple-element.441, f32[4,8,256]{2,1,0:T(8,128)S(1)} %select_maximum_fusion.2, ...), kind=kOutput, calls=%fused_computation.11.clone.1 | convolution fusion | flops 1094189056 | bytes 25886736 | tf_op jit(solution)/shard_map/while/body/eval_jaxpr/gjtb,bgd->gjtd/dot_general | solution.py:58
  155.5 9.7 %fusion.43 = f32[4,8,256]{2,1,0:T(8,128)S(1)} fusion(f32[4,512,256,8]{2,1,3,0:T(8,128)} %get-tuple-element.441, f32[4,8,256]{2,1,0:T(8,128)S(1)} %select_maximum_fusion.2, pred[256,512]{0,1:T(8,128)(4,1)S(1)} %compare_and_fusion.2), kind=kLoop, calls=%fused_computation.7.clone.1 | loop fusion | flops 16769024 | bytes 16973824 | tf_op jit(solution)/shard_map/while/body/eval_jaxpr/reduce_sum | solution.py:57
  165.2 11.4 %fusion.45 = f32[4,8,256,128]{3,2,1,0:T(8,128)} fusion(f32[4,8,256,128]{3,2,1,0:T(8,128)} %get-tuple-element.466, f32[4,8,256]{2,1,0:T(8,128)S(1)} %get-tuple-element.443, pred[]{:T(512)S(6)} %compare.3, f32[4,512,256,8]{2,1,3,0:T(8,128)} %get-tuple-element.441, f32[4,8,256]{2,1,0:T(8,128)S(1)} %select_maximum_fusion.2, ...), kind=kOutput, calls=%fused_computation.11.clone.1 | convolution fusion | flops 1094189056 | bytes 25886736 | tf_op jit(solution)/shard_map/while/body/eval_jaxpr/gjtb,bgd->gjtd/dot_general | solution.py:58
  186.4 9.2 %fusion.43 = f32[4,8,256]{2,1,0:T(8,128)S(1)} fusion(f32[4,512,256,8]{2,1,3,0:T(8,128)} %get-tuple-element.441, f32[4,8,256]{2,1,0:T(8,128)S(1)} %select_maximum_fusion.2, pred[256,512]{0,1:T(8,128)(4,1)S(1)} %compare_and_fusion.2), kind=kLoop, calls=%fused_computation.7.clone.1 | loop fusion | flops 16769024 | bytes 16973824 | tf_op jit(solution)/shard_map/while/body/eval_jaxpr/reduce_sum | solution.py:57
  195.6 11.0 %fusion.45 = f32[4,8,256,128]{3,2,1,0:T(8,128)} fusion(f32[4,8,256,128]{3,2,1,0:T(8,128)} %get-tuple-element.466, f32[4,8,256]{2,1,0:T(8,128)S(1)} %get-tuple-element.443, pred[]{:T(512)S(6)} %compare.3, f32[4,512,256,8]{2,1,3,0:T(8,128)} %get-tuple-element.441, f32[4,8,256]{2,1,0:T(8,128)S(1)} %select_maximum_fusion.2, ...), kind=kOutput, calls=%fused_computation.11.clone.1 | convolution fusion | flops 1094189056 | bytes 25886736 | tf_op jit(solution)/shard_map/while/body/eval_jaxpr/gjtb,bgd->gjtd/dot_general | solution.py:58
  216.4 9.4 %fusion.43 = f32[4,8,256]{2,1,0:T(8,128)S(1)} fusion(f32[4,512,256,8]{2,1,3,0:T(8,128)} %get-tuple-element.441, f32[4,8,256]{2,1,0:T(8,128)S(1)} %select_maximum_fusion.2, pred[256,512]{0,1:T(8,128)(4,1)S(1)} %compare_and_fusion.2), kind=kLoop, calls=%fused_computation.7.clone.1 | loop fusion | flops 16769024 | bytes 16973824 | tf_op jit(solution)/shard_map/while/body/eval_jaxpr/reduce_sum | solution.py:57
  225.8 11.2 %fusion.45 = f32[4,8,256,128]{3,2,1,0:T(8,128)} fusion(f32[4,8,256,128]{3,2,1,0:T(8,128)} %get-tuple-element.466, f32[4,8,256]{2,1,0:T(8,128)S(1)} %get-tuple-element.443, pred[]{:T(512)S(6)} %compare.3, f32[4,512,256,8]{2,1,3,0:T(8,128)} %get-tuple-element.441, f32[4,8,256]{2,1,0:T(8,128)S(1)} %select_maximum_fusion.2, ...), kind=kOutput, calls=%fused_computation.11.clone.1 | convolution fusion | flops 1094189056 | bytes 25886736 | tf_op jit(solution)/shard_map/while/body/eval_jaxpr/gjtb,bgd->gjtd/dot_general | solution.py:58
  246.5 9.8 %fusion.43 = f32[4,8,256]{2,1,0:T(8,128)S(1)} fusion(f32[4,512,256,8]{2,1,3,0:T(8,128)} %get-tuple-element.441, f32[4,8,256]{2,1,0:T(8,128)S(1)} %select_maximum_fusion.2, pred[256,512]{0,1:T(8,128)(4,1)S(1)} %compare_and_fusion.2), kind=kLoop, calls=%fused_computation.7.clone.1 | loop fusion | flops 16769024 | bytes 16973824 | tf_op jit(solution)/shard_map/while/body/eval_jaxpr/reduce_sum | solution.py:57
  256.3 11.5 %fusion.45 = f32[4,8,256,128]{3,2,1,0:T(8,128)} fusion(f32[4,8,256,128]{3,2,1,0:T(8,128)} %get-tuple-element.466, f32[4,8,256]{2,1,0:T(8,128)S(1)} %get-tuple-element.443, pred[]{:T(512)S(6)} %compare.3, f32[4,512,256,8]{2,1,3,0:T(8,128)} %get-tuple-element.441, f32[4,8,256]{2,1,0:T(8,128)S(1)} %select_maximum_fusion.2, ...), kind=kOutput, calls=%fused_computation.11.clone.1 | convolution fusion | flops 1094189056 | bytes 25886736 | tf_op jit(solution)/shard_map/while/body/eval_jaxpr/gjtb,bgd->gjtd/dot_general | solution.py:58
  277.5 9.6 %fusion.43 = f32[4,8,256]{2,1,0:T(8,128)S(1)} fusion(f32[4,512,256,8]{2,1,3,0:T(8,128)} %get-tuple-element.441, f32[4,8,256]{2,1,0:T(8,128)S(1)} %select_maximum_fusion.2, pred[256,512]{0,1:T(8,128)(4,1)S(1)} %compare_and_fusion.2), kind=kLoop, calls=%fused_computation.7.clone.1 | loop fusion | flops 16769024 | bytes 16973824 | tf_op jit(solution)/shard_map/while/body/eval_jaxpr/reduce_sum | solution.py:57
  287.1 11.3 %fusion.45 = f32[4,8,256,128]{3,2,1,0:T(8,128)} fusion(f32[4,8,256,128]{3,2,1,0:T(8,128)} %get-tuple-element.466, f32[4,8,256]{2,1,0:T(8,128)S(1)} %get-tuple-element.443, pred[]{:T(512)S(6)} %compare.3, f32[4,512,256,8]{2,1,3,0:T(8,128)} %get-tuple-element.441, f32[4,8,256]{2,1,0:T(8,128)S(1)} %select_maximum_fusion.2, ...), kind=kOutput, calls=%fused_computation.11.clone.1 | convolution fusion | flops 1094189056 | bytes 25886736 | tf_op jit(solution)/shard_map/while/body/eval_jaxpr/gjtb,bgd->gjtd/dot_general | solution.py:58
  308.2 9.2 %fusion.43 = f32[4,8,256]{2,1,0:T(8,128)S(1)} fusion(f32[4,512,256,8]{2,1,3,0:T(8,128)} %get-tuple-element.441, f32[4,8,256]{2,1,0:T(8,128)S(1)} %select_maximum_fusion.2, pred[256,512]{0,1:T(8,128)(4,1)S(1)} %compare_and_fusion.2), kind=kLoop, calls=%fused_computation.7.clone.1 | loop fusion | flops 16769024 | bytes 16973824 | tf_op jit(solution)/shard_map/while/body/eval_jaxpr/reduce_sum | solution.py:57
  317.5 11.1 %fusion.45 = f32[4,8,256,128]{3,2,1,0:T(8,128)} fusion(f32[4,8,256,128]{3,2,1,0:T(8,128)} %get-tuple-element.466, f32[4,8,256]{2,1,0:T(8,128)S(1)} %get-tuple-element.443, pred[]{:T(512)S(6)} %compare.3, f32[4,512,256,8]{2,1,3,0:T(8,128)} %get-tuple-element.441, f32[4,8,256]{2,1,0:T(8,128)S(1)} %select_maximum_fusion.2, ...), kind=kOutput, calls=%fused_computation.11.clone.1 | convolution fusion | flops 1094189056 | bytes 25886736 | tf_op jit(solution)/shard_map/while/body/eval_jaxpr/gjtb,bgd->gjtd/dot_general | solution.py:58
  338.2 9.5 %fusion.43 = f32[4,8,256]{2,1,0:T(8,128)S(1)} fusion(f32[4,512,256,8]{2,1,3,0:T(8,128)} %get-tuple-element.441, f32[4,8,256]{2,1,0:T(8,128)S(1)} %select_maximum_fusion.2, pred[256,512]{0,1:T(8,128)(4,1)S(1)} %compare_and_fusion.2), kind=kLoop, calls=%fused_computation.7.clone.1 | loop fusion | flops 16769024 | bytes 16973824 | tf_op jit(solution)/shard_map/while/body/eval_jaxpr/reduce_sum | solution.py:57
  347.7 11.6 %fusion.45 = f32[4,8,256,128]{3,2,1,0:T(8,128)} fusion(f32[4,8,256,128]{3,2,1,0:T(8,128)} %get-tuple-element.466, f32[4,8,256]{2,1,0:T(8,128)S(1)} %get-tuple-element.443, pred[]{:T(512)S(6)} %compare.3, f32[4,512,256,8]{2,1,3,0:T(8,128)} %get-tuple-element.441, f32[4,8,256]{2,1,0:T(8,128)S(1)} %select_maximum_fusion.2, ...), kind=kOutput, calls=%fused_computation.11.clone.1 | convolution fusion | flops 1094189056 | bytes 25886736 | tf_op jit(solution)/shard_map/while/body/eval_jaxpr/gjtb,bgd->gjtd/dot_general | solution.py:58
  367.4 73.3 %all-gather.8.cloned.1.call-done = bf16[4096,8192]{1,0:T(8,128)(2,1)} async-done(((bf16[256,8192]{1,0:T(8,128)(2,1)}), bf16[4096,8192]{1,0:T(8,128)(2,1)}) %all-gather.8.cloned.1.call-update) | async-done | bytes 67108880 | tf_op jit(solution)/shard_map/all_gather | solution.py:93
  440.7 28.3 %convolution_convert_fusion = bf16[256,8192]{1,0:T(8,128)(2,1)} fusion(bf16[256,4096]{0,1:T(8,128)(2,1)S(1)} %bitcast.108, bf16[4096,8192]{1,0:T(8,128)(2,1)} %all-gather.8.cloned.1.call-done), kind=kOutput, calls=%fused_computation.38 | convolution fusion | flops 17181966336 | bytes 73400320 | tf_op jit(solution)/shard_map/dot_general | solution.py:91
  471.5 32.6 %all-reduce = (f32[1,32]{1,0:T(1,128)S(1)}, f32[2,1,4]{2,0,1:T(2,128)S(1)}) all-reduce(f32[1,32]{1,0:T(1,128)S(1)} %bitcast.114, f32[2,1,4]{2,0,1:T(2,128)S(1)} %maximum_bitcast_fusion), channel_id=1, replica_groups=mesh['ctx'=16,'tp'=2] {'ctx'}, use_global_device_ids=true, to_apply=%region_9.10 | all-reduce | flops 40 | bytes 320 | tf_op jit(solution)/shard_map/pmax | solution.py:29
  505.5 18.1 %reduce-scatter.2.cloned.1.call-done = bf16[256,4096]{1,0:T(8,128)(2,1)} async-done(((bf16[256,8192]{1,0:T(8,128)(2,1)}), bf16[256,4096]{1,0:T(8,128)(2,1)}) %reduce-scatter.2.cloned.1.call-update) | async-done | bytes 2097168 | tf_op jit(solution)/shard_map/reduce_scatter | solution.py:96
  (126 shorter events, 94.5 us)
Async XLA Ops:
  7.2 56.2 %all-gather.4.cloned.1.call-start = ((), (), s32[]{:S(2)}) async-start(), calls=%async_computation.1 | async-start | bytes 4456448 | tf_op jit(solution)/shard_map/all_gather | solution.py:71
  7.9 106.5 %all-gather.6.cloned.1.call-start = ((), (), s32[]{:S(2)}) async-start(), calls=%async_computation.2 | async-start | bytes 4456448 | tf_op jit(solution)/shard_map/all_gather | solution.py:72
  8.6 4.1 copy-start.4
  8.7 432.0 %all-gather.8.cloned.1.call-start = ((), (), s32[]{:S(2)}) async-start(), calls=%async_computation.3 | async-start | bytes 71303168 | tf_op jit(solution)/shard_map/all_gather | solution.py:93
  9.4 514.2 %reduce-scatter.2.cloned.1.call-start = ((), (), s32[]{:S(2)}) async-start(), calls=%async_computation.4 | async-start | bytes 6291456 | tf_op jit(solution)/shard_map/reduce_scatter | solution.py:96
  12.8 1.4 copy-start
  14.2 4.6 copy-start.6
  469.0 0.9 copy-start.2
  469.0 1.1 copy-start.3
  469.0 1.8 copy-start.1
  469.0 35.9 %copy-start.5 = (f32[16,32]{1,0:T(8,128)S(1)}, f32[16,32]{1,0:T(8,128)}, u32[]{:S(2)}) copy-start(f32[16,32]{1,0:T(8,128)} %param.13) | copy-start | bytes 6148
Sparse Core Ops, SparseCore 0:
  10.1 53.1 all-gather.3
  65.5 48.8 all-gather.5
  116.0 324.6 all-gather.7
  469.2 54.3 reduce-scatter.1
where the time goes:
time: 531 us; the launch traced here: 530 us
  waiting for transfers between devices  188 us (35%)
  matrix products  179 us (34%)
  other arithmetic  84.3 us (16%)
  blocking collectives  32.6 us (6%)
  local copies, waits for them, and re-layouts  31.9 us (6%)
  between operations  13.9 us (3%)
    dot_general x8, matrix products, attend(): jnp.einsum('gjtb,bgd->gjtd', weights.astype(jnp.bfloat16), value_clip, pr...  89.3 us
    reduce_sum x8, other arithmetic, attend(): total = total * decay + jnp.sum(weights, axis=-1)  75.6 us
    all_gather x1, waiting for transfers between devices, on_device(): lax.all_gather(out_weight, 'ctx', axis=0, tiled=True)  73.3 us
    dot_general x8, matrix products, attend(): jnp.einsum('tgjd,bgd->gjtb', clipped, key_clip, preferred_element_type=jn...  61.2 us
    all_gather x1, waiting for transfers between devices, on_device(): value_piece = lax.all_gather(values, 'ctx', axis=0, tiled=True)  51.1 us
    all_gather x1, waiting for transfers between devices, on_device(): key_piece = lax.all_gather(keys, 'ctx', axis=0, tiled=True)  43.7 us
    pmax x1, blocking collectives, on_device(): lax.pmax((query_peak, jnp.stack([key_peak, value_peak])), 'ctx')  32.6 us
    dot_general x1, matrix products, on_device(): jnp.dot(attn, lax.all_gather(out_weight, 'ctx', axis=0, tiled=True), pref...  28.3 us
  transfers between devices with their start and end apart: 4, of which 4 were waited for; matrix products, arithmetic and copies ran while one was open for 50% of the time, Pallas kernels for 0%

commit v1 on v0

v1 whole, which is shorter than its diff:
```python
import functools
import math

import jax
import jax.numpy as jnp
from jax import lax
from jax.experimental import pallas as pl
from jax.experimental.pallas import tpu as pltpu
from jax.sharding import PartitionSpec as P

NEG = -1e30


def attend_kernel(
    low_ref, high_ref, base_ref, q_ref, k_ref, v_ref, start_ref, o_ref, acc_ref, top_ref,
    *, stacks, stack, head_size, block, scale
):
    number = pl.program_id(0)
    rows = q_ref.shape[1]
    tall = stack * rows
    row_pos = base_ref[number] + lax.broadcasted_iota(jnp.int32, (rows, block), 0)
    row_start = start_ref[0]
    acc_ref[...] = jnp.zeros_like(acc_ref)
    top_ref[...] = jnp.full_like(top_ref, NEG)
    queries = []
    for part in range(stacks):
        heads = [
            q_ref[0, :, (part * stack + j) * head_size : (part * stack + j + 1) * head_size]
            for j in range(stack)
        ]
        queries.append(jnp.concatenate(heads, axis=0))

    def step(key_number, carry):
        key_first = pl.multiple_of(key_number * block, block)
        keys = k_ref[pl.ds(key_first, block), :]
        values = v_ref[pl.ds(key_first, block), :]
        key_pos = key_first + lax.broadcasted_iota(jnp.int32, (rows, block), 1)
        bias = jnp.where((key_pos <= row_pos) & (key_pos >= row_start), 0.0, NEG)
        for part in range(stacks):
            scores = lax.dot_general(
                queries[part], keys, (((1,), (1,)), ((), ())), preferred_element_type=jnp.float32
            )
            scores = (scores.reshape(stack, rows, block) * scale + bias[None]).reshape(tall, block)
            old_top = top_ref[part]
            top = jnp.maximum(old_top, jnp.max(scores, axis=1, keepdims=True))
            weights = jnp.exp2(scores - top[:, :1]).astype(jnp.bfloat16)
            decay = jnp.exp2(old_top - top)
            top_ref[part] = top
            product = jnp.dot(weights, values, preferred_element_type=jnp.float32)
            acc_ref[part] = acc_ref[part] * jnp.concatenate([decay, decay], axis=1) + product
        return carry

    lax.fori_loop(low_ref[number], high_ref[number], step, 0)
    for part in range(stacks):
        result = acc_ref[part, :, :head_size] / acc_ref[part, :, head_size:]
        for j in range(stack):
            first = (part * stack + j) * head_size
            o_ref[0, :, first : first + head_size] = result[j * rows : (j + 1) * rows].astype(
                o_ref.dtype
            )


def attend(queries, keys, values, starts, bases, chunk, rows, head_size):
    groups, _, width = queries.shape
    heads = width // head_size
    stack = math.gcd(heads, 4)
    stacks = math.gcd(heads // stack, 2)
    per_step = stack * stacks
    tokens = keys.shape[0]
    block = math.gcd(tokens, 512)
    low = starts[:, 0, 0] // block
    high = (bases + rows - 1) // block + 1
    kernel = functools.partial(
        attend_kernel, stacks=stacks, stack=stack, head_size=head_size, block=block,
        scale=math.log2(math.e) / math.sqrt(head_size),
    )
    spec = pltpu.PrefetchScalarGridSpec(
        num_scalar_prefetch=3,
        grid=(groups, heads // per_step),
        in_specs=[
            pl.BlockSpec((1, rows, per_step * head_size), lambda g, h, *_: (g, chunk, h)),
            pl.BlockSpec((tokens, head_size), lambda g, h, *_: (0, 0)),
            pl.BlockSpec((tokens, 2 * head_size), lambda g, h, *_: (0, 0)),
            pl.BlockSpec((1, rows, 1), lambda g, h, *_: (g, 0, 0)),
        ],
        out_specs=pl.BlockSpec((1, rows, per_step * head_size), lambda g, h, *_: (g, 0, h)),
        scratch_shapes=[
            pltpu.VMEM((stacks, stack * rows, 2 * head_size), jnp.float32),
            pltpu.VMEM((stacks, stack * rows, head_size), jnp.float32),
        ],
    )
    return pl.pallas_call(
        kernel,
        grid_spec=spec,
        out_shape=jax.ShapeDtypeStruct((groups, rows, width), jnp.bfloat16),
        compiler_params=pltpu.CompilerParams(vmem_limit_bytes=40 * 2**20),
        cost_estimate=pl.CostEstimate(
            flops=groups * rows * width * tokens * 2,
            bytes_accessed=groups * rows * width * 4,
            transcendentals=groups * rows * heads * tokens // 2,
        ),
    )(low, high, bases, queries, keys, values, starts)


def on_device(
    queries, keys, values, documents, hist_q, hist_kv, out_weight, *, ctx, tp, groups, chunks
):
    rows_here, width = queries.shape
    kv_heads = hist_kv.shape[2]
    heads_here = hist_q.shape[1]
    group = heads_here // kv_heads
    head_size = width // heads_here
    near = ctx // groups
    far_sets = [[g * near + n for g in range(groups)] for n in range(near)]
    near_sets = [[g * near + n for n in range(near)] for g in range(groups)]
    place = lax.axis_index("ctx")
    mine = lax.axis_index("tp")
    far, close = place // near, place % near
    columns = out_weight.shape[1] // tp

    def passed(array, shift):
        return lax.ppermute(array, "tp", [(t, (t + shift) % tp) for t in range(tp)])

    def weight_columns(owner):
        return lax.dynamic_slice_in_dim(out_weight, owner * columns, columns, axis=1)

    query_limit = jnp.max(hist_q, axis=0)
    pair_limit = jnp.max(hist_kv, axis=1)

    def clip(array, limit):
        wide = jnp.repeat(limit, head_size)[None, :]
        return jnp.clip(array.astype(jnp.float32), -wide, wide).astype(jnp.bfloat16)

    leaving = [weight_columns((mine + shift) % tp) for shift in range(tp)]

    def gathered(piece):
        return lax.all_gather(piece, "ctx", axis=0, axis_index_groups=near_sets, tiled=True)

    keys_in, leaving[0] = lax.optimization_barrier((keys, leaving[0]))
    weights = [gathered(leaving[0])]
    arrived = [passed(leaving[shift], shift) for shift in range(1, tp)]
    key_clip, value_clip = clip(keys_in, pair_limit[0]), clip(values, pair_limit[1])
    tokens = documents.shape[0]
    if kv_heads % groups == 0:
        kv_here = kv_heads // groups
        part = kv_here * head_size
        both = jnp.concatenate(
            [key_clip.reshape(rows_here, groups, part), value_clip.reshape(rows_here, groups, part)],
            axis=2,
        )
        both = jnp.transpose(both, (1, 0, 2))
        both = lax.all_to_all(both, "ctx", 0, 0, axis_index_groups=far_sets, tiled=True)
        both, weights[0], *arrived = lax.optimization_barrier((both, weights[0], *arrived))
        both = lax.all_gather(both, "ctx", axis=0, axis_index_groups=near_sets)
        both = jnp.transpose(both, (1, 0, 2, 3)).reshape(tokens, 2 * part)
        key_all, value_all = both[:, :part], both[:, part:]
        kv_first = [j for j in range(kv_here)]
    else:
        kv_here = 1
        both = lax.all_gather(
            jnp.concatenate([key_clip, value_clip], axis=1), "ctx", axis=0, tiled=True
        )
        head = far * (heads_here // groups) // group
        key_all = lax.dynamic_slice_in_dim(both, head * head_size, head_size, axis=1)
        value_all = lax.dynamic_slice_in_dim(
            both, (kv_heads + head) * head_size, head_size, axis=1
        )
        kv_first = [0]
    query_clip = clip(queries, query_limit)
    query_part = width // groups
    query_all = jnp.transpose(query_clip.reshape(rows_here, groups, query_part), (1, 0, 2))
    query_all = lax.all_to_all(query_all, "ctx", 0, 0, axis_index_groups=far_sets, tiled=True)

    weights += [gathered(piece) for piece in arrived]

    rows = rows_here // chunks
    share = query_part // kv_here
    ones = jnp.ones((tokens, head_size), jnp.bfloat16)
    outs = []
    for chunk in range(chunks):
        bases = (jnp.arange(groups, dtype=jnp.int32) * near + close) * rows_here + chunk * rows
        row_pos = bases[:, None] + jnp.arange(rows, dtype=jnp.int32)[None, :]
        row_docs = documents.reshape(groups, near, rows_here)
        row_docs = lax.dynamic_index_in_dim(row_docs, close, 1, keepdims=False)
        row_docs = row_docs[:, chunk * rows : (chunk + 1) * rows]
        starts = jnp.sum(
            (documents[None, None, :] < row_docs[:, :, None]).astype(jnp.int32), axis=2
        )[:, :, None]
        pieces = []
        for j in kv_first:
            own = slice(j * head_size, (j + 1) * head_size)
            pieces.append(
                attend(
                    query_all[:, :, j * share : (j + 1) * share],
                    key_all[:, own],
                    jnp.concatenate([value_all[:, own], ones], axis=1),
                    starts, bases, chunk, rows, head_size,
                )
            )
        attn = pieces[0] if len(pieces) == 1 else jnp.concatenate(pieces, axis=2)
        attn = attn.reshape(groups * rows, query_part)
        total = jnp.dot(attn, weights[0], preferred_element_type=jnp.float32)
        for shift in range(1, tp):
            total = total + jnp.dot(
                passed(attn, shift), weights[shift], preferred_element_type=jnp.float32
            )
        outs.append(
            lax.psum_scatter(
                total.astype(jnp.bfloat16), "ctx", scatter_dimension=0,
                axis_index_groups=far_sets, tiled=True,
            )
        )
    mixed = jnp.concatenate(outs, axis=0)

    def peak(array, heads):
        size = jnp.abs(array.astype(jnp.float32).reshape(rows_here, heads, head_size))
        return jnp.max(size, axis=(0, 2))

    current_query, current_pair = lax.pmax(
        (peak(queries, heads_here), jnp.stack([peak(keys, kv_heads), peak(values, kv_heads)])),
        "ctx",
    )
    new_hist_q = jnp.concatenate([current_query[None], hist_q[:-1]], axis=0)
    new_hist_kv = jnp.concatenate([current_pair[:, None], hist_kv[:, :-1]], axis=1)
    return (mixed, new_hist_q, new_hist_kv)


def solution(mesh):
    ctx, tp = mesh.shape["ctx"], mesh.shape["tp"]
    groups = max(ctx // 4, 1)
    in_specs = (
        P("ctx", "tp"),
        P("ctx", "tp"),
        P("ctx", "tp"),
        P(),
        P(None, "tp"),
        P(None, None, "tp"),
        P(("tp", "ctx"), None),
    )
    out_specs = (P("ctx", "tp"), P(None, "tp"), P(None, None, "tp"))
    body = functools.partial(on_device, ctx=ctx, tp=tp, groups=groups, chunks=2)
    return jax.shard_map(
        body, mesh=mesh, in_specs=in_specs, out_specs=out_specs, check_vma=False
    )
```

time: 531 us -> 362 us (0.68)
  matrix products: 179 us -> 32 us
  other arithmetic: 84.3 us -> 11.7 us
  Pallas kernels: 0 us -> 27.5 us
  blocking collectives: 32.6 us -> 49.5 us
  starting transfers between devices: 0.15 us -> 11 us
  local copies, waits for them, and re-layouts: 31.9 us -> 22.4 us
    all_gather x3, waiting for transfers between devices: 168 us -> 16.6 us  [the longest x2 12.3 us: gathered(): lax.all_gather(piece, 'ctx', axis=0, axis_index_groups=near_sets, tiled=T...]
    dot_general x17 -> x4, matrix products: 179 us -> 32 us  [the longest x2 18 us: on_device(): total = jnp.dot(attn, weights[0], preferred_element_type=jnp.float32)]
    reduce_sum x8 -> x1, other arithmetic: 75.6 us -> 1.94 us  [on_device(): jnp.sum((documents[None, None, :] < row_docs[:, :, None]).astype(jnp.int3...]
    ppermute x0 -> x3, waiting for transfers between devices: none -> 70.5 us  [passed(): return lax.ppermute(array, 'tp', [(t, (t + shift) % tp) for t in range(tp)])]
    reduce_scatter x1 -> x2, waiting for transfers between devices: 18.1 us -> 65.8 us  [on_device(): lax.psum_scatter(total.astype(jnp.bfloat16), 'ctx', scatter_dimension=0,...]
    all_to_all x0 -> x1, waiting for transfers between devices: none -> 38.4 us  [on_device(): lax.all_to_all(query_all, 'ctx', 0, 0, axis_index_groups=far_sets, tiled=...]
    pallas_call x0 -> x2, Pallas kernels: none -> 27.5 us  [attend(): pl.pallas_call(kernel, grid_spec=spec, out_shape=jax.ShapeDtypeStruct((gr...]
    all_to_all x0 -> x1, blocking collectives: none -> 18.9 us  [on_device(): lax.all_to_all(both, 'ctx', 0, 0, axis_index_groups=far_sets, tiled=True)]
  transfers between devices with their start and end apart: 4 -> 9, of which waited for: 4 -> 7; matrix products, arithmetic and copies ran while one was open for 50% -> 10% of each run, Pallas kernels for 0% -> 8%
where the time goes in v1:
time: 362 us; the launch traced here: 360 us
  waiting for transfers between devices  192 us (53%)
  blocking collectives  49.5 us (14%)
  matrix products  32 us (9%)
  Pallas kernels  27.5 us (8%)
  local copies, waits for them, and re-layouts  22.4 us (6%)
  between operations  14.1 us (4%)
  other arithmetic  11.7 us (3%)
  starting transfers between devices  11 us (3%)
    ppermute x3, waiting for transfers between devices, passed(): return lax.ppermute(array, 'tp', [(t, (t + shift) % tp) for t in range(tp)])  70.5 us
    reduce_scatter x2, waiting for transfers between devices, on_device(): lax.psum_scatter(total.astype(jnp.bfloat16), 'ctx', scatter_dimension=0,...  65.8 us
    all_to_all x1, waiting for transfers between devices, on_device(): lax.all_to_all(query_all, 'ctx', 0, 0, axis_index_groups=far_sets, tiled=...  38.4 us
    pmax x1, blocking collectives, on_device(): lax.pmax((peak(queries, heads_here), jnp.stack([peak(keys, kv_heads), pea...  30.6 us
    pallas_call x2, Pallas kernels, attend(): pl.pallas_call(kernel, grid_spec=spec, out_shape=jax.ShapeDtypeStruct((gr...  27.5 us
    all_to_all x1, blocking collectives, on_device(): lax.all_to_all(both, 'ctx', 0, 0, axis_index_groups=far_sets, tiled=True)  18.9 us
    dot_general x2, matrix products, on_device(): total = jnp.dot(attn, weights[0], preferred_element_type=jnp.float32)  18 us
    dot_general x2, matrix products, on_device(): jnp.dot(passed(attn, shift), weights[shift], preferred_element_type=jnp.f...  13.9 us
  transfers between devices with their start and end apart: 9, of which 7 were waited for; matrix products, arithmetic and copies ran while one was open for 10% of the time, Pallas kernels for 8%

profile of v1, /device:TPU:0, one launch (start us, length us, event | category | flops | bytes accessed | tf_op | source)
XLA Modules:
  0.0 360.2 jit_solution(1339988903632132236)
XLA Ops:
  7.3 4.0 %constant_dynamic-slice_fusion = (bf16[256,4096]{1,0:T(8,128)(2,1)S(1)}, bf16[256,4096]{1,0:T(8,128)(2,1)}) fusion(bf16[256,8192]{1,0:T(8,128)(2,1)} %param.13, s32[]{:T(128)S(6)} %select_n.47, s32[]{:T(128)S(6)} %select_n.45), kind=kLoop, calls=%fused_computation.49 | loop fusion | bytes 8388616 | tf_op jit(solution)/shard_map/dynamic_slice | solution.py:125
  11.3 3.1 collective-permute-start
  15.4 18.9 %all_to_all.10 = bf16[4,256,256]{1,2,0:T(8,128)(2,1)S(1)} all-to-all(bf16[4,256,256]{1,2,0:T(8,128)(2,1)S(1)} %maximum_bitcast_fusion), channel_id=1, replica_groups={{0,8,16,24},{2,10,18,26},{4,12,20,28},{6,14,22,30},{1,9,17,25},{3,11,19..., dimensions={0} | all-to-all | bytes 1048576 | tf_op jit(solution)/shard_map/all_to_all | solution.py:152
  34.3 25.8 %collective-permute-done = bf16[256,4096]{1,0:T(8,128)(2,1)} collective-permute-done((bf16[256,4096]{1,0:T(8,128)(2,1)S(1)}, bf16[256,4096]{1,0:T(8,128)(2,1)}, u32[]{:S(2)}, u32[]{:S(2)}) %collective-permute-start) | collective-permute-done | bytes 2097184 | tf_op jit(solution)/shard_map/ppermute | solution.py:122
  60.1 12.3 %all-gather.5.cloned.1.call-done = bf16[1024,4096]{1,0:T(8,128)(2,1)} async-done(((bf16[256,4096]{1,0:T(8,128)(2,1)}), bf16[1024,4096]{1,0:T(8,128)(2,1)}) %all-gather.5.cloned.1.call-update) | async-done | bytes 8388624 | tf_op jit(solution)/shard_map/all_gather | solution.py:137
  74.3 3.3 copy.35
  77.7 3.4 fusion.1
  81.1 4.1 %copy.36 = bf16[256,4,1024]{2,0,1:T(8,128)(2,1)} copy(bf16[256,4,1024]{0,2,1:T(8,128)(2,1)} %bitcast.57) | data formatting | bytes 4194304 | tf_op jit(solution)/shard_map/reshape | solution.py:171
  85.2 4.5 %all-to-all-start = ((bf16[4,256,1024]{2,1,0:T(8,128)(2,1)}), bf16[4,256,1024]{2,1,0:T(8,128)(2,1)S(1)}, u32[]{:S(2)}, u32[]{:S(2)}) async-start(bf16[4,256,1024]{2,1,0:T(8,128)(2,1)} %bitcast.55), calls=%async_computation | async-start | bytes 4194304 | tf_op jit(solution)/shard_map/all_to_all | solution.py:172
  89.8 1.9 convert_reduce_fusion.1
  92.2 4.3 %all-gather.9.cloned.1.call-done = bf16[16,256,256]{2,1,0:T(8,128)(2,1)} async-done(((bf16[4,256,256]{2,1,0:T(8,128)(2,1)}), bf16[16,256,256]{2,1,0:T(8,128)(2,1)}) %all-gather.9.cloned.1.call-update) | async-done | bytes 2097168 | tf_op jit(solution)/shard_map/all_gather | solution.py:154
  96.6 1.7 copy.40
  100.0 38.4 %all-to-all-done.q_ref = bf16[4,256,1024]{2,1,0:T(8,128)(2,1)S(1)} async-done(((bf16[4,256,1024]{2,1,0:T(8,128)(2,1)}), bf16[4,256,1024]{2,1,0:T(8,128)(2,1)S(1)}, u32[]{:S(2)}, u32[]{:S(2)}) %all-to-all-start) | async-done | bytes 2097184 | tf_op jit(solution)/shard_map/all_to_all | solution.py:172
  140.1 13.7 %shard_map.95 = bf16[4,128,1024]{2,1,0:T(8,128)(2,1)S(1)} custom-call(s32[4]{0:T(128)S(1)} %get-tuple-element.25.low_ref, s32[4]{0:T(128)S(1)} %get-tuple-element.27.high_ref, s32[4]{0:T(128)S(1)} %get-tuple-element.30.base_ref, bf16[4,256,1024]{2,1,0:T(8,128)(2,1)S(1)} %all-to-all-done.q_ref, bf16[4096,128]{1,0:T(8,128)(2,1)S(1)} %get-tuple-element.20.k_ref, ...), custom_call_target="tpu_custom_call" | custom-call | flops 4294967296 | bytes 2097152 | tf_op jit(solution)/shard_map/pallas_call | solution.py:92
  156.2 22.8 %collective-permute-done.2 = bf16[512,1024]{1,0:T(8,128)(2,1)} collective-permute-done((bf16[512,1024]{1,0:T(8,128)(2,1)S(1)}, bf16[512,1024]{1,0:T(8,128)(2,1)}, u32[]{:S(2)}, u32[]{:S(2)}) %collective-permute-start.2) | collective-permute-done | bytes 1048608 | tf_op jit(solution)/shard_map/ppermute | solution.py:122
  179.0 7.3 %fusion.11 = f32[512,4096]{1,0:T(8,128)S(1)} fusion(bf16[512,1024]{1,0:T(8,128)(2,1)} %collective-permute-done.2, bf16[1024,4096]{1,0:T(8,128)(2,1)} %all-gather.7.cloned.1.call-done), kind=kOutput, calls=%fused_computation.61 | convolution fusion | flops 4294967296 | bytes 17825792 | tf_op jit(solution)/shard_map/dot_general | solution.py:204
  186.3 9.7 %add_convert_fusion = bf16[512,4096]{1,0:T(8,128)(2,1)} fusion(f32[512,4096]{1,0:T(8,128)S(1)} %fusion.11, bf16[512,1024]{1,0:T(8,128)(2,1)S(1)} %bitcast.54, bf16[1024,4096]{1,0:T(8,128)(2,1)} %all-gather.5.cloned.1.call-done), kind=kOutput, calls=%fused_computation | convolution fusion | flops 4299161600 | bytes 22020096 | tf_op jit(solution)/shard_map/dot_general | solution.py:202
  198.0 13.8 %shard_map.94 = bf16[4,128,1024]{2,1,0:T(8,128)(2,1)S(1)} custom-call(s32[4]{0:T(128)S(1)} %get-tuple-element.26.low_ref, s32[4]{0:T(128)S(1)} %get-tuple-element.28.high_ref, s32[4]{0:T(128)S(1)} %get-tuple-element.29.base_ref, bf16[4,256,1024]{2,1,0:T(8,128)(2,1)S(1)} %all-to-all-done.q_ref, bf16[4096,128]{1,0:T(8,128)(2,1)S(1)} %get-tuple-element.20.k_ref, ...), custom_call_target="tpu_custom_call" | custom-call | flops 4294967296 | bytes 2097152 | tf_op jit(solution)/shard_map/pallas_call | solution.py:92
  213.4 21.9 %collective-permute-done.1 = bf16[512,1024]{1,0:T(8,128)(2,1)S(1)} collective-permute-done((bf16[512,1024]{1,0:T(8,128)(2,1)S(1)}, bf16[512,1024]{1,0:T(8,128)(2,1)S(1)}, u32[]{:S(2)}, u32[]{:S(2)}) %collective-permute-start.1) | collective-permute-done | bytes 1048608 | tf_op jit(solution)/shard_map/ppermute | solution.py:122
  235.3 6.7 %fusion.10 = f32[512,4096]{1,0:T(8,128)} fusion(bf16[512,1024]{1,0:T(8,128)(2,1)S(1)} %collective-permute-done.1, bf16[1024,4096]{1,0:T(8,128)(2,1)S(1)} %copy-done.14), kind=kOutput, calls=%fused_computation.60 | convolution fusion | flops 4294967296 | bytes 17825792 | tf_op jit(solution)/shard_map/dot_general | solution.py:204
  242.0 8.4 %add_convert_fusion.1 = bf16[512,4096]{1,0:T(8,128)(2,1)} fusion(f32[512,4096]{1,0:T(8,128)} %fusion.10, bf16[512,1024]{1,0:T(8,128)(2,1)S(1)} %bitcast.52, bf16[1024,4096]{1,0:T(8,128)(2,1)S(1)} %bitcast.72), kind=kOutput, calls=%fused_computation.2 | convolution fusion | flops 4299161600 | bytes 22020096 | tf_op jit(solution)/shard_map/dot_general | solution.py:202
  252.8 30.6 %all-reduce.1 = (f32[1,32]{1,0:T(1,128)S(1)}, f32[2,1,4]{2,0,1:T(2,128)S(1)}) all-reduce(f32[1,32]{1,0:T(1,128)S(1)} %bitcast.70, f32[2,1,4]{2,0,1:T(2,128)S(1)} %maximum_bitcast_fusion.1), channel_id=1, replica_groups=mesh['ctx'=16,'tp'=2] {'ctx'}, use_global_device_ids=true, to_apply=%region_8.9 | all-reduce | flops 40 | bytes 320 | tf_op jit(solution)/shard_map/pmax | solution.py:219
  284.8 65.8 %reduce-scatter.3.cloned.1.call-done = bf16[128,4096]{1,0:T(8,128)(2,1)} async-done(((bf16[512,4096]{1,0:T(8,128)(2,1)}), bf16[128,4096]{1,0:T(8,128)(2,1)}) %reduce-scatter.3.cloned.1.call-update) | async-done | bytes 1048592 | tf_op jit(solution)/shard_map/reduce_scatter | solution.py:208
  350.6 3.1 pad_maximum_fusion
  (85 shorter events, 16.7 us)
Async XLA Ops:
  7.2 65.3 %all-gather.5.cloned.1.call-start = ((), (), s32[]{:S(2)}) async-start(), calls=%async_computation.4 | async-start | bytes 10485760 | tf_op jit(solution)/shard_map/all_gather | solution.py:137
  7.2 7.2 %copy-start.10 = (bf16[256,512]{1,0:T(8,128)(2,1)S(1)}, bf16[256,512]{1,0:T(8,128)(2,1)}, u32[]{:S(2)}) copy-start(bf16[256,512]{1,0:T(8,128)(2,1)} %param.9) | copy-start | bytes 786436
  7.2 7.3 %copy-start.8 = (bf16[256,512]{1,0:T(8,128)(2,1)S(1)}, bf16[256,512]{1,0:T(8,128)(2,1)}, u32[]{:S(2)}) copy-start(bf16[256,512]{1,0:T(8,128)(2,1)} %param.8) | copy-start | bytes 786436
  7.3 7.4 %copy-start.12 = (f32[2,16,4]{1,2,0:T(4,128)S(1)}, f32[2,16,4]{1,2,0:T(4,128)}, u32[]{:S(2)}) copy-start(f32[2,16,4]{1,2,0:T(4,128)} %param.12) | copy-start | bytes 1540
  11.3 63.0 %copy-start.11 = (f32[16,32]{1,0:T(8,128)S(1)}, f32[16,32]{1,0:T(8,128)}, u32[]{:S(2)}) copy-start(f32[16,32]{1,0:T(8,128)} %param.11) | copy-start | bytes 6148
  11.3 85.3 %all-gather.9.cloned.1.call-start = ((), (), s32[]{:S(2)}) async-start(), calls=%async_computation.8 | async-start | bytes 2621440 | tf_op jit(solution)/shard_map/all_gather | solution.py:154
  11.3 48.8 %collective-permute-start = (bf16[256,4096]{1,0:T(8,128)(2,1)S(1)}, bf16[256,4096]{1,0:T(8,128)(2,1)}, u32[]{:S(2)}, u32[]{:S(2)}) collective-permute-start(bf16[256,4096]{1,0:T(8,128)(2,1)S(1)} %get-tuple-element.17), channel_id=1, source_target_pairs={{0,1},{1,0},{2,3},{3,2},{4,5},{5,4},{6,7},{7,6},{8,9},{9,8},{10,11... | collective-permute-start | bytes 6291464 | tf_op jit(solution)/shard_map/ppermute | solution.py:122
  14.6 59.7 %copy-start.6 = (bf16[256,512]{0,1:T(8,128)(2,1)}, bf16[256,512]{0,1:T(8,128)(2,1)S(1)}, u32[]{:S(2)}) copy-start(bf16[256,512]{0,1:T(8,128)(2,1)S(1)} %copy.38) | copy-start | bytes 786436
  73.5 105.6 %all-gather.7.cloned.1.call-start = ((), (), s32[]{:S(2)}) async-start(), calls=%async_computation.5 | async-start | bytes 10485760 | tf_op jit(solution)/shard_map/all_gather | solution.py:137
  77.5 7.7 %copy-start.4 = (bf16[256,4096]{0,1:T(8,128)(2,1)}, bf16[256,4096]{0,1:T(8,128)(2,1)S(1)}, u32[]{:S(2)}) copy-start(bf16[256,4096]{0,1:T(8,128)(2,1)S(1)} %copy.35) | copy-start | bytes 6291460
  81.1 8.6 %copy-start.13 = (s32[4096]{0:T(1024)S(1)}, s32[4096]{0:T(1024)}, u32[]{:S(2)}) copy-start(s32[4096]{0:T(1024)} %param.10) | copy-start | bytes 49156
  85.2 53.2 %all-to-all-start = ((bf16[4,256,1024]{2,1,0:T(8,128)(2,1)}), bf16[4,256,1024]{2,1,0:T(8,128)(2,1)S(1)}, u32[]{:S(2)}, u32[]{:S(2)}) async-start(bf16[4,256,1024]{2,1,0:T(8,128)(2,1)} %bitcast.55), calls=%async_computation | async-start | bytes 4194304 | tf_op jit(solution)/shard_map/all_to_all | solution.py:172
  89.8 195.0 %reduce-scatter.5.cloned.1.call-start = ((), (), s32[]{:S(2)}) async-start(), calls=%async_computation.7 | async-start | bytes 5242880 | tf_op jit(solution)/shard_map/reduce_scatter | solution.py:208
  138.4 1.7 copy-start
  154.7 24.3 %collective-permute-start.2 = (bf16[512,1024]{1,0:T(8,128)(2,1)S(1)}, bf16[512,1024]{1,0:T(8,128)(2,1)}, u32[]{:S(2)}, u32[]{:S(2)}) collective-permute-start(bf16[512,1024]{1,0:T(8,128)(2,1)S(1)} %bitcast.53), channel_id=1, source_target_pairs={{0,1},{1,0},{2,3},{3,2},{4,5},{5,4},{6,7},{7,6},{8,9},{9,8},{10,11... | collective-permute-start | bytes 3145736 | tf_op jit(solution)/shard_map/ppermute | solution.py:122
  179.0 7.3 %copy-start.3 = (bf16[4,128,1024]{2,1,0:T(8,128)(2,1)S(1)}, bf16[4,128,1024]{2,1,0:T(8,128)(2,1)}, u32[]{:S(2)}) copy-start(bf16[4,128,1024]{2,1,0:T(8,128)(2,1)} %copy-done.2) | copy-start | bytes 3145732
  196.1 154.5 %reduce-scatter.3.cloned.1.call-start = ((), (), s32[]{:S(2)}) async-start(), calls=%async_computation.6 | async-start | bytes 5242880 | tf_op jit(solution)/shard_map/reduce_scatter | solution.py:208
  196.4 1.6 copy-start.1
  198.0 37.3 %copy-start.14 = (bf16[1024,4096]{1,0:T(8,128)(2,1)S(1)}, bf16[1024,4096]{1,0:T(8,128)(2,1)}, u32[]{:S(2)}) copy-start(bf16[1024,4096]{1,0:T(8,128)(2,1)} %all-gather.7.cloned.1.call-done) | copy-start | bytes 25165828
  211.9 30.1 %slice-start = ((s8[8388608]{0:T(1024)(128)(4,1)}), s8[4194304]{0:T(1024)(128)(4,1)S(1)}, s32[]{:S(2)}) async-start(s8[8388608]{0:T(1024)(128)(4,1)} %bitcast.71), calls=%async_computation.9 | async-start | bytes 8388608
  211.9 30.1 %slice-start.1 = ((s8[8388608]{0:T(1024)(128)(4,1)}), s8[4194304]{0:T(1024)(128)(4,1)S(1)}, s32[]{:S(2)}) async-start(s8[8388608]{0:T(1024)(128)(4,1)} %bitcast.71), calls=%async_computation.10 | async-start | bytes 8388608
  211.9 23.4 %collective-permute-start.1 = (bf16[512,1024]{1,0:T(8,128)(2,1)S(1)}, bf16[512,1024]{1,0:T(8,128)(2,1)S(1)}, u32[]{:S(2)}, u32[]{:S(2)}) collective-permute-start(bf16[512,1024]{1,0:T(8,128)(2,1)S(1)} %bitcast.51), channel_id=1, source_target_pairs={{0,1},{1,0},{2,3},{3,2},{4,5},{5,4},{6,7},{7,6},{8,9},{9,8},{10,11... | collective-permute-start | bytes 3145736 | tf_op jit(solution)/shard_map/ppermute | solution.py:122
  250.3 1.1 copy-start.7
  250.3 1.8 copy-start.5
  (2 other events, 1.9 us)
Sparse Core Ops, SparseCore 0:
  11.4 60.9 all-gather.4
  74.0 22.5 all-gather.8
  98.1 58.2 all-gather.6
  196.2 75.0 reduce-scatter.4
  273.4 77.1 reduce-scatter.2
